TPU v7x, 32 devices: a whole 2x2x4 slice. The times are simulated.
32 devices in a mesh: grp: 2 (over x), dap: 16 (over z, y, core).
Axes of the slice: x: 2, y: 2, z: 4, core: 2. Of those that a mesh axis runs over, the one named last changes fastest.
Arguments:
- homolog_stack_tensor: bfloat16 [64, 64, 256], P(('grp', 'dap')), parts along dimension 0, may hold values from -6.5 to 6.5
- occupancy_indicator: int32 [64, 64], P('grp'), parts along dimension 0, may hold values from 0 to 1, as said below
- chain_existence_flags: int32 [64], P('grp'), parts along dimension 0, may hold values from 0 to 1, as said below
- focus_normal_factor: float32 [256], replicated, may hold values from 0.25 to 1.75
- focus_normal_addend: float32 [256], replicated, may hold values from -3 to 3
- probe_index_weights: bfloat16 [256, 512], replicated, may hold values from -3 to 3
- payload_valve_weights: bfloat16 [256, 512], replicated, may hold values from -0.375 to 0.375
- logistic_valve_addend: float32 [256], replicated, may hold values from -4 to 4
- focus_exit_weights: bfloat16 [256, 256], replicated, may hold values from -0.375 to 0.375
- focus_exit_addend: float32 [256], replicated, may hold values from -3 to 3
- product_mean_layer_stretch: float32 [256], replicated, may hold values from 0.25 to 1.75
- product_mean_layer_shift: float32 [256], replicated, may hold values from -2 to 2
- twin_map_matrix: bfloat16 [256, 64], replicated, may hold values from -0.375 to 0.375
- twin_map_shift: float32 [64], replicated, may hold values from -2 to 2
- couple_map_matrix: bfloat16 [1024, 128], replicated, may hold values from -0.75 to 0.75
- couple_map_shift: float32 [128], replicated, may hold values from -3 to 3
Outputs:
- alignment_after: bfloat16 [64, 64, 256], P('grp', 'dap'), parts along dimension 0
- pair_features_after: bfloat16 [128, 64, 128], P(('grp', 'dap')), parts along dimension 0
There are 2 independent parts, one for each index of `grp`. A program takes and returns all parts, laid end to end along the dimension named above; an argument that names none is the same for every part. Nothing has to cross between parts.
Inputs may be any that keep to these rules, and one draw needn't show every extreme that they name: `chain_existence_flags`: 1 for the first 16 sequences, 0 for the last one. `occupancy_indicator`: every sequence is 0 from some residue on (the last residue always, never more than the last 32); before it sequence 0 is all 1 and the others have gaps.
All inputs are finite; a program needn't handle non-finite values.
Results may differ from a plain program's by a relative error of at most 0.008.
Values may be sent and summed in bfloat16 or wider, within the bound.
A program may use at most 64 MiB of HBM per device.

v0:
```python
import jax
import jax.numpy as jnp
from jax import lax
from jax.sharding import PartitionSpec as P

HEAD_COUNT = 8
HEAD_CHANNELS = 32
OUTER_CHANNELS = 32
PAIR_DIM = 128


EPSILON = 1e-05
MASKED = -100000.0


def layer_norm(value_vectors, scale_vec, shift_vec):
    widened = value_vectors.astype(jnp.float32)
    centred = widened - jnp.mean(widened, axis=-1, keepdims=True)
    variance = jnp.mean(centred * centred, axis=-1, keepdims=True)
    scaled = centred * lax.rsqrt(variance + EPSILON)
    return (scaled * scale_vec + shift_vec).astype(jnp.bfloat16)


def heed_across_lanes(
    vertical_pieces,
    present_mask,
    focus_normal_factor,
    focus_normal_addend,
    probe_index_weights,
    payload_valve_weights,
    logistic_valve_addend,
    focus_exit_weights,
    focus_exit_addend,
):
    seq_count, res_count, feature_width = vertical_pieces.shape
    inner_channel_width = HEAD_COUNT * HEAD_CHANNELS
    normed = layer_norm(vertical_pieces, focus_normal_factor, focus_normal_addend).reshape(
        seq_count * res_count, feature_width
    )
    query_key = jnp.dot(normed, probe_index_weights, preferred_element_type=jnp.float32)
    value_gate = jnp.dot(normed, payload_valve_weights, preferred_element_type=jnp.float32)
    head_shape = (seq_count, res_count, HEAD_COUNT, HEAD_CHANNELS)
    query_rows_all = (
        (query_key[:, :inner_channel_width] * HEAD_CHANNELS ** (-0.5))
        .astype(jnp.bfloat16)
        .reshape(head_shape)
    )
    key_rows = query_key[:, inner_channel_width:].astype(jnp.bfloat16).reshape(head_shape)
    value_rows = value_gate[:, :inner_channel_width].astype(jnp.bfloat16).reshape(head_shape)
    gating = jax.nn.sigmoid(value_gate[:, inner_channel_width:] + logistic_valve_addend)
    scores = jnp.einsum(
        "srhd,trhd->rhst", query_rows_all, key_rows, preferred_element_type=jnp.float32
    )
    allowed = jnp.transpose(present_mask > 0)[:, None, None, :]
    scores = jnp.where(allowed, scores, MASKED)
    exponent = jnp.exp(scores - jnp.max(scores, axis=-1, keepdims=True))
    weights = (exponent / jnp.sum(exponent, axis=-1, keepdims=True)).astype(jnp.bfloat16)
    attended = jnp.einsum(
        "rhst,trhd->srhd", weights, value_rows, preferred_element_type=jnp.float32
    )
    gated_rows = (attended.reshape(seq_count * res_count, inner_channel_width) * gating).astype(
        jnp.bfloat16
    )
    update = (
        jnp.dot(gated_rows, focus_exit_weights, preferred_element_type=jnp.float32)
        + focus_exit_addend
    )
    return (
        vertical_pieces.astype(jnp.float32) + update.reshape(seq_count, res_count, feature_width)
    ).astype(jnp.bfloat16)


def project_pairs(
    revised_tensor,
    present_mask,
    product_mean_layer_stretch,
    product_mean_layer_shift,
    twin_map_matrix,
    twin_map_shift,
):
    seq_count, res_count, feature_width = revised_tensor.shape
    normed = layer_norm(
        revised_tensor, product_mean_layer_stretch, product_mean_layer_shift
    ).reshape(seq_count * res_count, feature_width)
    projected = (
        jnp.dot(normed, twin_map_matrix, preferred_element_type=jnp.float32) + twin_map_shift
    )
    projected = projected.reshape(seq_count, res_count, 2 * OUTER_CHANNELS) * present_mask[
        :, :, None
    ].astype(jnp.float32)
    projected = projected.astype(jnp.bfloat16)
    return (projected[:, :, :OUTER_CHANNELS], projected[:, :, OUTER_CHANNELS:])


def pair_tile(left_rows, right_cols, live_rows, live_cols, couple_map_matrix, couple_map_shift):
    row_count = left_rows.shape[1]
    col_count = right_cols.shape[1]
    outer_sum = jnp.einsum(
        "sic,sje->ijce", left_rows, right_cols, preferred_element_type=jnp.float32
    )
    counts = jnp.einsum("si,sj->ij", live_rows, live_cols, preferred_element_type=jnp.float32)
    mean_terms = (
        outer_sum.reshape(row_count, col_count, OUTER_CHANNELS * OUTER_CHANNELS)
        / jnp.maximum(counts, 1.0)[:, :, None]
    ).astype(jnp.bfloat16)
    result = jnp.dot(
        mean_terms.reshape(row_count * col_count, OUTER_CHANNELS * OUTER_CHANNELS),
        couple_map_matrix,
        preferred_element_type=jnp.float32,
    )
    result = result + couple_map_shift
    return result.astype(jnp.bfloat16).reshape(row_count, col_count, PAIR_DIM)


def tiled_pairs(left_rows, right_cols, live_rows, live_cols, couple_map_matrix, couple_map_shift):
    return pair_tile(
        left_rows, right_cols, live_rows, live_cols, couple_map_matrix, couple_map_shift
    )


def shards(
    homolog_stack_tensor,
    occupancy_indicator,
    chain_existence_flags,
    focus_normal_factor,
    focus_normal_addend,
    probe_index_weights,
    payload_valve_weights,
    logistic_valve_addend,
    focus_exit_weights,
    focus_exit_addend,
    product_mean_layer_stretch,
    product_mean_layer_shift,
    twin_map_matrix,
    twin_map_shift,
    couple_map_matrix,
    couple_map_shift,
):
    vertical_pieces = lax.all_to_all(
        homolog_stack_tensor, "dap", split_axis=1, concat_axis=0, tiled=True
    )
    seq_count, res_local, feature_width = vertical_pieces.shape
    position = lax.axis_index("dap")
    present_integer = occupancy_indicator * chain_existence_flags[:, None]
    live_all = present_integer.astype(jnp.bfloat16)
    live_own = lax.dynamic_slice_in_dim(present_integer, position * res_local, res_local, 1)
    revised_tensor = heed_across_lanes(
        vertical_pieces,
        live_own,
        focus_normal_factor,
        focus_normal_addend,
        probe_index_weights,
        payload_valve_weights,
        logistic_valve_addend,
        focus_exit_weights,
        focus_exit_addend,
    )
    left_own, right_own = project_pairs(
        revised_tensor,
        live_own,
        product_mean_layer_stretch,
        product_mean_layer_shift,
        twin_map_matrix,
        twin_map_shift,
    )
    live_rows = live_own.astype(jnp.bfloat16)
    pair_rows = tiled_pairs(
        left_own,
        lax.all_gather(right_own, "dap", axis=1, tiled=True),
        live_rows,
        live_all,
        couple_map_matrix,
        couple_map_shift,
    )
    return (revised_tensor, pair_rows)


def solution(mesh):
    in_specs = (
        P(("grp", "dap"), None, None),
        P("grp", None),
        P("grp"),
        P(),
        P(),
        P(),
        P(),
        P(),
        P(),
        P(),
        P(),
        P(),
        P(),
        P(),
        P(),
        P(),
    )
    out_specs = (P("grp", "dap", None), P(("grp", "dap"), None, None))
    return jax.shard_map(shards, mesh=mesh, in_specs=in_specs, out_specs=out_specs, check_vma=False)
```

profile of v0, /device:TPU:0, one launch (start us, length us, event | category | flops | bytes accessed | tf_op | source)
XLA Modules:
  0.0 49.4 jit_solution(6411777289907106998)
XLA Ops:
  0.6 1.6 %copy.54 = bf16[2,64,256]{2,0,1:T(2,128)(2,1)} copy(bf16[2,64,256]{2,1,0:T(8,128)(2,1)} %param.16) | data formatting | bytes 131072 | tf_op args[0]
  2.2 7.4 %all-to-all-start = ((bf16[2,64,256]{2,0,1:T(2,128)(2,1)}), bf16[2,64,256]{2,0,1:T(2,128)(2,1)S(1)}, u32[]{:S(2)}, u32[]{:S(2)}) async-start(bf16[2,64,256]{2,0,1:T(2,128)(2,1)} %copy.54), calls=%async_computation | async-start | bytes 131072 | tf_op jit(solution)/shard_map/all_to_all | solution.py:139
  9.7 0.8 %copy.56 = s32[32,64]{0,1:T(8,128)S(1)} copy(s32[32,64]{1,0:T(8,128)} %param.17) | data formatting | bytes 16384 | tf_op args[1]
  10.4 0.7 %broadcast_multiply_fusion = s32[32,64]{0,1:T(8,128)S(1)} fusion(s32[32,64]{0,1:T(8,128)S(1)} %copy.56, s32[32]{0:T(128)} %param.18), kind=kLoop, calls=%fused_computation.50 | loop fusion | flops 2048 | bytes 16512 | tf_op jit(solution)/shard_map/mul | solution.py:144
  11.1 0.1 convolution_maximum_fusion
  11.3 5.2 %all-to-all-done = bf16[2,64,256]{2,0,1:T(2,128)(2,1)S(1)} async-done(((bf16[2,64,256]{2,0,1:T(2,128)(2,1)}), bf16[2,64,256]{2,0,1:T(2,128)(2,1)S(1)}, u32[]{:S(2)}, u32[]{:S(2)}) %all-to-all-start) | async-done | bytes 65568 | tf_op jit(solution)/shard_map/all_to_all | solution.py:139
  16.6 0.1 bitcast_reduce_fusion
  16.7 0.1 div.37
  16.8 0.2 multiply_reduce_fusion
  17.2 0.1 rsqrt.20
  17.3 1.0 %fusion.38 = f32[128,512]{1,0:T(8,128)S(1)} fusion(bf16[256,512]{1,0:T(8,128)(2,1)S(1)} %copy-done, f32[128,256]{1,0:T(8,128)S(1)} %reshape.129, f32[256]{0:T(256)} %param.20, f32[256]{0:T(256)} %param.19, f32[128]{0:T(128)S(1)} %rsqrt.20, f32[128]{0:T(128)S(1)} %div.37), kind=kOutput, calls=%fused_computation.63 | convolution fusion | flops 33718272 | bytes 658432 | tf_op jit(solution)/shard_map/dot_general | solution.py:40
  18.4 0.2 reshape.121
  18.5 0.2 reshape.122
  18.7 0.3 fusion.40
  19.1 0.3 convolution_select_fusion
  19.4 0.2 fusion.39
  19.6 0.2 reshape.120
  19.9 0.3 convolution_bitcast_fusion.1
  20.3 0.5 copy.61
  20.7 0.2 reshape.123
  20.9 0.3 convert_reduce_fusion
  21.2 0.2 fusion.10
  21.5 0.2 convolution_add_fusion.2
  21.7 0.1 copy.62
  22.0 0.7 %reshape.124 = f32[32,4,256]{2,1,0:T(4,128)} reshape(f32[128,256]{1,0:T(8,128)S(1)} %get-tuple-element.4) | data formatting | bytes 262144 | tf_op jit(solution)/shard_map/reshape | solution.py:69
  22.7 19.1 %all_gather.3 = bf16[32,64,32]{2,0,1:T(8,128)(2,1)S(1)} all-gather(bf16[32,4,32]{2,0,1:T(8,128)(2,1)S(1)} %copy.64), channel_id=1, replica_groups=mesh['grp'=2,'dap'=16] {'dap'}, dimensions={1}, use_global_device_ids=true | all-gather | bytes 139264 | tf_op jit(solution)/shard_map/all_gather | solution.py:169
  41.9 0.9 %copy.68 = bf16[32,64,32,1]{0,1,3,2:T(8,128)(2,1)S(1)} copy(bf16[32,64,32,1]{2,0,1,3:T(8,128)(2,1)S(1)} %bitcast.36) | data formatting | bytes 262144 | tf_op jit(solution)/shard_map/all_gather | solution.py:169
  42.7 0.7 %convolution_bitcast_fusion = f32[4,64,32,32]{1,2,0,3:T(8,128)S(1)} fusion(bf16[32,64,32,1]{0,1,3,2:T(8,128)(2,1)S(1)} %copy.68, bf16[32,4,64]{0,2,1:T(8,128)(2,1)S(1)} %multiply_convert_fusion), kind=kOutput, calls=%fused_computation.1 | convolution fusion | flops 16777216 | bytes 1605632 | tf_op jit(solution)/shard_map/sic,sje->ijce/dot_general | solution.py:98
  43.4 1.4 %copy.66 = f32[4,64,32,32]{1,0,3,2:T(4,128)S(1)} copy(f32[4,64,32,32]{1,2,0,3:T(8,128)S(1)} %convolution_bitcast_fusion) | data formatting | bytes 2097152 | tf_op jit(solution)/shard_map/sic,sje->ijce/transpose | solution.py:98
  44.8 1.1 %reshape.126 = f32[256,1024]{0,1:T(8,128)S(1)} reshape(f32[4,64,32,32]{1,0,3,2:T(4,128)S(1)} %copy.66) | data formatting | bytes 2097152 | tf_op jit(solution)/shard_map/reshape | solution.py:103
  45.9 1.6 %fusion.20 = bf16[32,4,256]{2,1,0:T(4,128)(2,1)} fusion(f32[32,4,256]{2,1,0:T(4,128)} %reshape.124, f32[2,16,4,256]{3,2,0,1:T(4,128)S(1)} %copy.55), kind=kLoop, calls=%fused_computation.36 | loop fusion | flops 65536 | bytes 327680 | tf_op jit(solution)/shard_map/convert_element_type | solution.py:70
  47.5 1.9 %fusion.3 = bf16[256,128]{1,0:T(8,128)(2,1)} fusion(bf16[1024,128]{1,0:T(8,128)(2,1)} %param.30, f32[256,1024]{0,1:T(8,128)S(1)} %reshape.126, f32[256]{0:T(256)S(1)} %div.44, f32[128]{0:T(128)S(1)} %copy-done.11), kind=kOutput, calls=%fused_computation.8 | convolution fusion | flops 67698688 | bytes 1377792 | tf_op jit(solution)/shard_map/dot_general | solution.py:106
  (42 shorter events, 0.6 us)
Async XLA Ops:
  0.6 16.7 %copy-start = (bf16[256,512]{1,0:T(8,128)(2,1)S(1)}, bf16[256,512]{1,0:T(8,128)(2,1)}, u32[]{:S(2)}) copy-start(bf16[256,512]{1,0:T(8,128)(2,1)} %param.21) | copy-start | bytes 786436
  2.2 14.3 %all-to-all-start = ((bf16[2,64,256]{2,0,1:T(2,128)(2,1)}), bf16[2,64,256]{2,0,1:T(2,128)(2,1)S(1)}, u32[]{:S(2)}, u32[]{:S(2)}) async-start(bf16[2,64,256]{2,0,1:T(2,128)(2,1)} %copy.54), calls=%async_computation | async-start | bytes 131072 | tf_op jit(solution)/shard_map/all_to_all | solution.py:139
  17.3 2.1 %copy-start.1 = (bf16[256,512]{1,0:T(8,128)(2,1)S(1)}, bf16[256,512]{1,0:T(8,128)(2,1)}, u32[]{:S(2)}) copy-start(bf16[256,512]{1,0:T(8,128)(2,1)} %param.22) | copy-start | bytes 786436
  17.3 2.1 %copy-start.2 = (f32[256]{0:T(256)S(1)}, f32[256]{0:T(256)}, u32[]{:S(2)}) copy-start(f32[256]{0:T(256)} %param.20) | copy-start | bytes 3076
  17.3 2.1 %copy-start.3 = (f32[256]{0:T(256)S(1)}, f32[256]{0:T(256)}, u32[]{:S(2)}) copy-start(f32[256]{0:T(256)} %param.19) | copy-start | bytes 3076
  19.8 1.1 %copy-start.4 = (bf16[256,256]{1,0:T(8,128)(2,1)S(1)}, bf16[256,256]{1,0:T(8,128)(2,1)}, u32[]{:S(2)}) copy-start(bf16[256,256]{1,0:T(8,128)(2,1)} %param.24) | copy-start | bytes 393220
  19.8 1.1 %copy-start.6 = (f32[256]{0:T(256)S(1)}, f32[256]{0:T(256)}, u32[]{:S(2)}) copy-start(f32[256]{0:T(256)} %param.25) | copy-start | bytes 3076
  19.8 1.1 %copy-start.7 = (f32[256]{0:T(256)S(1)}, f32[256]{0:T(256)}, u32[]{:S(2)}) copy-start(f32[256]{0:T(256)} %param.23) | copy-start | bytes 3076
  19.9 1.6 %copy-start.5 = (bf16[256,64]{0,1:T(8,128)(2,1)S(1)}, bf16[256,64]{0,1:T(8,128)(2,1)}, u32[]{:S(2)}) copy-start(bf16[256,64]{0,1:T(8,128)(2,1)} %param.28) | copy-start | bytes 98308
  19.9 1.6 %copy-start.8 = (f32[256]{0:T(256)S(1)}, f32[256]{0:T(256)}, u32[]{:S(2)}) copy-start(f32[256]{0:T(256)} %param.27) | copy-start | bytes 3076
  19.9 1.6 %copy-start.9 = (f32[256]{0:T(256)S(1)}, f32[256]{0:T(256)}, u32[]{:S(2)}) copy-start(f32[256]{0:T(256)} %param.26) | copy-start | bytes 3076
  19.9 1.6 %copy-start.10 = (f32[64]{0:T(128)S(1)}, f32[64]{0:T(128)}, u32[]{:S(2)}) copy-start(f32[64]{0:T(128)} %param.29) | copy-start | bytes 772
  44.8 2.7 %copy-start.11 = (f32[128]{0:T(128)S(1)}, f32[128]{0:T(128)}, u32[]{:S(2)}) copy-start(f32[128]{0:T(128)} %param.31) | copy-start | bytes 1540
where the time goes:
time: 49.8 us; the launch traced here: 49.4 us
  blocking collectives  19.1 us (38%)
  local copies, waits for them, and re-layouts  8.33 us (17%)
  starting transfers between devices  7.41 us (15%)
  matrix products  5.4 us (11%)
  waiting for transfers between devices  5.2 us (10%)
  other arithmetic  2.89 us (6%)
  between operations  1.03 us (2%)
    all_gather x1, blocking collectives, shards(): lax.all_gather(right_own, 'dap', axis=1, tiled=True)  19.1 us
    all_to_all x1, starting transfers between devices, shards(): lax.all_to_all(homolog_stack_tensor, 'dap', split_axis=1, concat_axis=0,...  7.41 us
    all_to_all x1, waiting for transfers between devices, shards(): lax.all_to_all(homolog_stack_tensor, 'dap', split_axis=1, concat_axis=0,...  5.2 us
    unnamed x26, local copies, waits for them, and re-layouts  2.46 us
    dot_general x1, matrix products, pair_tile(): jnp.dot(mean_terms.reshape(row_count * col_count, OUTER_CHANNELS * OUTER_...  1.93 us
    convert_element_type x1, other arithmetic, heed_across_lanes(): return (vertical_pieces.astype(jnp.float32) + update.reshape(seq_count, r...  1.58 us
    transpose x1, local copies, waits for them, and re-layouts, pair_tile(): jnp.einsum('sic,sje->ijce', left_rows, right_cols, preferred_element_type...  1.35 us
    reshape x1, local copies, waits for them, and re-layouts, pair_tile(): outer_sum.reshape(row_count, col_count, OUTER_CHANNELS * OUTER_CHANNELS)  1.13 us
  transfers between devices with their start and end apart: 1, of which 1 were waited for; matrix products, arithmetic and copies ran while one was open for 3% of the time, Pallas kernels for 0%

commit v1 on v0

v1 whole, which is shorter than its diff:
```python
import functools

import jax
import jax.numpy as jnp
from jax import lax
from jax.experimental import pallas as pl
from jax.experimental.pallas import tpu as pltpu
from jax.sharding import PartitionSpec as P

HEAD_COUNT = 8
HEAD_CHANNELS = 32
OUTER_CHANNELS = 32
PAIR_DIM = 128
EPSILON = 1e-05
MASKED = -100000.0
OTHER = -3.0e38
CHUNK = 128

F32 = jnp.float32
BF16 = jnp.bfloat16
MESH = pl.DeviceIdType.MESH


def iota(shape, dim):
    return lax.broadcasted_iota(jnp.int32, shape, dim)


def dot(a, b):
    return jnp.dot(a, b, preferred_element_type=F32)


def dot_t(a, b):
    return lax.dot_general(a, b, (((1,), (1,)), ((), ())), preferred_element_type=F32)


def layer_norm(x, scale, shift):
    centred = x - jnp.mean(x, axis=-1, keepdims=True)
    variance = jnp.mean(centred * centred, axis=-1, keepdims=True)
    return (centred * lax.rsqrt(variance + EPSILON) * scale + shift).astype(BF16)


def repeat(count, body):
    if count == 1:
        body(0)
    else:
        lax.fori_loop(0, count, lambda i, c: (body(i), c)[1], 0)


def each_peer(n, body):
    if n <= 16:
        for k in range(1, n):
            body(k)
    else:
        lax.fori_loop(1, n, lambda k, c: (body(k), c)[1], 0)


def kernel(
    n,
    x_ref, occ_ref, flag_ref, ng_ref, na_ref, wqk_hbm, wvg_hbm, gb_ref, wo_hbm, ob_ref,
    pg_ref, pa_ref, wt_ref, bt_ref, cm_hbm, cb_ref,
    out_ref, pair_ref,
    send, recv, rsend, rbuf, wqk, wvg, wo, cm, cmf, w2,
    q_s, kb_s, vb_s, g_s, t_s, inv_s, live_s,
    wsem, ssem, rsem, ssem2, rsem2,
):
    me = lax.axis_index("dap")
    own, res, width = x_ref.shape
    local = res // n
    seqs = occ_ref.shape[0]
    tokens = seqs * local
    chunks = tokens // CHUNK
    per = CHUNK // local
    ke = OUTER_CHANNELS * per

    loads = [
        pltpu.make_async_copy(src, dst, wsem.at[i])
        for i, (src, dst) in enumerate(
            ((cm_hbm, cm), (wqk_hbm, wqk), (wvg_hbm, wvg), (wo_hbm, wo))
        )
    ]
    for load in loads:
        load.start()

    barrier = pltpu.get_barrier_semaphore()

    def greet(k):
        pl.semaphore_signal(
            barrier, inc=1, device_id={"dap": lax.rem(me + k, n)}, device_id_type=MESH
        )

    each_peer(n, greet)

    x32 = x_ref[...].astype(F32)
    for p in range(n):
        rows = [x32[s, local * p : local * (p + 1)] for s in range(own)]
        send[p] = jnp.concatenate(rows, axis=0).astype(BF16)
    recv[me] = send[me]

    pl.semaphore_wait(barrier, n - 1)

    def post(k):
        peer = lax.rem(me + k, n)
        pltpu.make_async_remote_copy(
            src_ref=send.at[peer],
            dst_ref=recv.at[me],
            send_sem=ssem,
            recv_sem=rsem,
            device_id={"dap": peer},
            device_id_type=MESH,
        ).start()

    each_peer(n, post)

    occ = occ_ref[...].astype(F32)
    flag = flag_ref[...].astype(F32)
    pick = (iota((8, res), 1) == me * local + iota((8, res), 0)).astype(F32)
    pick = jnp.where(iota((8, res), 0) < local, pick, 0.0)
    live_rs = dot_t(pick, occ) * flag
    owner = (iota((seqs, tokens), 0) == iota((seqs, tokens), 1) // local).astype(F32)
    live_rt = dot(live_rs, owner)
    same = iota((8, tokens), 0) == lax.rem(iota((8, tokens), 1), local)
    live_row = jnp.sum(jnp.where(same, live_rt, 0.0), axis=0, keepdims=True)
    counts = dot(live_rs, occ)
    eye = (iota((res, res), 0) == iota((res, res), 1)).astype(F32)
    counts_t = lax.dot_general(
        eye, counts, (((1,), (1,)), ((), ())),
        precision=lax.Precision.HIGHEST, preferred_element_type=F32,
    )
    inv_s[...] = 1.0 / jnp.maximum(counts_t, 1.0)

    def live_column(ch):
        token = iota((CHUNK, seqs), 0)
        mine = (token // local + ch * per == iota((CHUNK, seqs), 1)).astype(F32) * flag
        spread = dot(mine, occ)
        here = iota((CHUNK, res), 1) == me * local + lax.rem(iota((CHUNK, res), 0), local)
        live_s[pl.ds(ch * CHUNK, CHUNK), :] = jnp.sum(
            jnp.where(here, spread, 0.0), axis=1, keepdims=True
        )

    repeat(chunks, live_column)

    loads[0].wait()
    cmf[...] = cm[...].astype(F32)
    for e in range(OUTER_CHANNELS):
        w2[0:OUTER_CHANNELS, e * PAIR_DIM : (e + 1) * PAIR_DIM] = cmf[
            pl.ds(e, OUTER_CHANNELS, stride=OUTER_CHANNELS), :
        ].astype(BF16)
    w2[OUTER_CHANNELS:, :] = jnp.zeros((OUTER_CHANNELS, OUTER_CHANNELS * PAIR_DIM), BF16)

    spread_e = (
        iota((2 * OUTER_CHANNELS, ke), 0) == OUTER_CHANNELS + iota((2 * OUTER_CHANNELS, ke), 1) // per
    ).astype(BF16)
    own_seq = iota((CHUNK, ke), 0) // local == lax.rem(iota((CHUNK, ke), 1), per)
    sel = (iota((8, CHUNK), 0) == lax.rem(iota((8, CHUNK), 1), local)).astype(BF16)
    perm_row = iota((CHUNK, CHUNK), 0)
    perm = (
        iota((CHUNK, CHUNK), 1) == lax.rem(perm_row, per) * local + perm_row // per
    ).astype(BF16)
    lane_head = iota((CHUNK, width), 1) // HEAD_CHANNELS

    for load in loads[1:]:
        load.wait()
    pltpu.make_async_copy(recv.at[pl.ds(0, n - 1)], recv.at[pl.ds(0, n - 1)], rsem).wait()

    block = own * local
    blocks = CHUNK // block

    def token_rows(ch):
        return recv[pl.ds(ch * blocks, blocks)].astype(F32).reshape(CHUNK, width)

    def project(ch):
        normed = layer_norm(token_rows(ch), ng_ref[...], na_ref[...])
        qk = dot(normed, wqk[...])
        vg = dot(normed, wvg[...])
        at = pl.ds(ch * CHUNK, CHUNK)
        q_s[at, :] = (qk[:, :width] * HEAD_CHANNELS**-0.5).astype(BF16)
        k = qk[:, width:].astype(BF16)
        v = vg[:, :width].astype(BF16)
        zero = jnp.zeros_like(k)
        one = jnp.ones_like(k)
        for h in range(HEAD_COUNT):
            row = pl.ds(h * tokens + ch * CHUNK, CHUNK)
            kb_s[row, :] = jnp.where(lane_head == h, k, zero)
            vb_s[row, 0:width] = jnp.where(lane_head == h, v, zero)
            vb_s[row, width:] = jnp.where(lane_head == h, one, zero)
        g_s[at, :] = jax.nn.sigmoid(vg[:, width:] + gb_ref[...])

    repeat(chunks, project)

    def attend(ch):
        at = pl.ds(ch * CHUNK, CHUNK)
        q = q_s[at, :]
        alive = live_row > 0.0
        mate = lax.rem(iota((CHUNK, tokens), 0), local) == lax.rem(iota((CHUNK, tokens), 1), local)
        probs = []
        for h in range(HEAD_COUNT):
            scores = dot_t(q, kb_s[h * tokens : (h + 1) * tokens, :])
            scores = jnp.where(mate, jnp.where(alive, scores, MASKED), OTHER)
            probs.append(
                jnp.exp(scores - jnp.max(scores, axis=-1, keepdims=True)).astype(BF16)
            )
        both = dot(jnp.concatenate(probs, axis=1), vb_s[...])
        attended = both[:, :width] / both[:, width:]
        gated = (attended * g_s[at, :]).astype(BF16)
        update = dot(gated, wo[...]) + ob_ref[...]
        after = token_rows(ch) + update
        revised = after.astype(BF16)
        out_ref[pl.ds(ch * per, per)] = after.reshape(per, local, width).astype(BF16)
        normed = layer_norm(revised.astype(F32), pg_ref[...], pa_ref[...])
        projected = (dot(normed, wt_ref[...]) + bt_ref[...]) * live_s[at, :]
        projected = projected.astype(BF16)
        wide = jnp.where(own_seq, dot(projected, spread_e), 0.0).astype(BF16)
        mine = dot(sel, wide)[:local].astype(BF16)
        if chunks == 1:
            rsend[...] = mine
        else:
            rsend[:, pl.ds(pl.multiple_of(ch * ke, ke), ke)] = mine
        if chunks == 1:
            post_right()
        left = dot(perm, projected).astype(BF16)
        for e in range(OUTER_CHANNELS):
            part = dot(left, w2[:, e * PAIR_DIM : (e + 1) * PAIR_DIM]).astype(BF16)
            for i in range(local):
                t_s[ch, e * per : (e + 1) * per, i * PAIR_DIM : (i + 1) * PAIR_DIM] = part[
                    i * per : (i + 1) * per
                ]

    def post_right():
        rbuf[me] = rsend[...]

        def post(k):
            pltpu.make_async_remote_copy(
                src_ref=rsend,
                dst_ref=rbuf.at[me],
                send_sem=ssem2,
                recv_sem=rsem2,
                device_id={"dap": lax.rem(me + k, n)},
                device_id_type=MESH,
            ).start()

        each_peer(n, post)

    repeat(chunks, attend)
    if chunks > 1:
        post_right()

    pltpu.make_async_copy(rbuf.at[pl.ds(0, n - 1)], rbuf.at[pl.ds(0, n - 1)], rsem2).wait()

    total = None
    for ch in range(chunks):
        right = rbuf[:, :, ch * ke : (ch + 1) * ke].astype(F32).reshape(res, ke).astype(BF16)
        part = dot(right, t_s[ch])
        total = part if total is None else total + part
    inv = inv_s[...]
    for i in range(local):
        pair_ref[i] = (
            total[:, i * PAIR_DIM : (i + 1) * PAIR_DIM] * inv[:, i : i + 1] + cb_ref[...]
        ).astype(BF16)

    pltpu.make_async_copy(send.at[pl.ds(0, n - 1)], send.at[pl.ds(0, n - 1)], ssem).wait()
    pltpu.make_async_copy(rbuf.at[pl.ds(0, n - 1)], rbuf.at[pl.ds(0, n - 1)], ssem2).wait()


def shards(n, *args):
    x, occ, flag, ng, na, wqk, wvg, gb, wo, ob, pg, pa, wt, bt, cm, cb = args
    own, res, width = x.shape
    local = res // n
    seqs = occ.shape[0]
    tokens = seqs * local
    chunks = tokens // CHUNK
    ke = OUTER_CHANNELS * (CHUNK // local)
    row = lambda v: v.reshape(1, -1)
    vm = pl.BlockSpec(memory_space=pltpu.VMEM)
    hbm = pl.BlockSpec(memory_space=pl.ANY)
    return pl.pallas_call(
        functools.partial(kernel, n),
        out_shape=(
            jax.ShapeDtypeStruct((seqs, local, width), BF16),
            jax.ShapeDtypeStruct((local, res, PAIR_DIM), BF16),
        ),
        in_specs=[vm, vm, vm, vm, vm, hbm, hbm, vm, hbm, vm, vm, vm, vm, vm, hbm, vm],
        out_specs=(vm, vm),
        scratch_shapes=[
            pltpu.VMEM((n, own * local, width), BF16),
            pltpu.VMEM((n, own * local, width), BF16),
            pltpu.VMEM((local, chunks * ke), BF16),
            pltpu.VMEM((n, local, chunks * ke), BF16),
            pltpu.VMEM(wqk.shape, BF16),
            pltpu.VMEM(wvg.shape, BF16),
            pltpu.VMEM(wo.shape, BF16),
            pltpu.VMEM(cm.shape, BF16),
            pltpu.VMEM(cm.shape, F32),
            pltpu.VMEM((2 * OUTER_CHANNELS, OUTER_CHANNELS * PAIR_DIM), BF16),
            pltpu.VMEM((tokens, width), BF16),
            pltpu.VMEM((HEAD_COUNT * tokens, width), BF16),
            pltpu.VMEM((HEAD_COUNT * tokens, 2 * width), BF16),
            pltpu.VMEM((tokens, width), F32),
            pltpu.VMEM((chunks, ke, local * PAIR_DIM), BF16),
            pltpu.VMEM((res, 8), F32),
            pltpu.VMEM((tokens, 1), F32),
            pltpu.SemaphoreType.DMA((4,)),
            pltpu.SemaphoreType.DMA,
            pltpu.SemaphoreType.DMA,
            pltpu.SemaphoreType.DMA,
            pltpu.SemaphoreType.DMA,
        ],
        compiler_params=pltpu.CompilerParams(
            collective_id=0, has_side_effects=True, vmem_limit_bytes=60 * 1024 * 1024
        ),
        name="evoformer",
    )(x, occ, row(flag), row(ng), row(na), wqk, wvg, row(gb), wo, row(ob),
      row(pg), row(pa), wt, row(bt), cm, row(cb))


def solution(mesh):
    in_specs = (P(("grp", "dap"), None, None), P("grp", None), P("grp")) + (P(),) * 13
    out_specs = (P("grp", "dap", None), P(("grp", "dap"), None, None))
    return jax.shard_map(
        functools.partial(shards, mesh.shape["dap"]),
        mesh=mesh, in_specs=in_specs, out_specs=out_specs, check_vma=False,
    )
```

time: 49.8 us -> 22.8 us (0.46)
  blocking collectives: 19.1 us -> 0 us
  Pallas kernels: 0 us -> 18.2 us
  starting transfers between devices: 7.41 us -> 0 us
  matrix products: 5.4 us -> 0 us
  waiting for transfers between devices: 5.2 us -> 0 us
  local copies, waits for them, and re-layouts: 8.33 us -> 3.65 us
  other arithmetic: 2.89 us -> 0 us
    all_gather x1 -> x0, blocking collectives: 19.1 us -> none  [shards(): lax.all_gather(right_own, 'dap', axis=1, tiled=True)]
    pallas_call x0 -> x1, Pallas kernels: none -> 18.2 us  [shards(): pl.pallas_call(functools.partial(kernel, n), out_shape=(jax.ShapeDtypeStr...]
    all_to_all x1 -> x0, starting transfers between devices: 7.41 us -> none  [shards(): lax.all_to_all(homolog_stack_tensor, 'dap', split_axis=1, concat_axis=0,...]
    all_to_all x1 -> x0, waiting for transfers between devices: 5.2 us -> none  [shards(): lax.all_to_all(homolog_stack_tensor, 'dap', split_axis=1, concat_axis=0,...]
    dot_general x9 -> x0, matrix products: 5.06 us -> none  [the longest x1 1.93 us: pair_tile(): jnp.dot(mean_terms.reshape(row_count * col_count, OUTER_CHANNELS * OUTER_...]
    reshape x7 -> x0, local copies, waits for them, and re-layouts: 2.58 us -> none  [the longest x1 1.13 us: pair_tile(): outer_sum.reshape(row_count, col_count, OUTER_CHANNELS * OUTER_CHANNELS)]
    transpose x2 -> x0, local copies, waits for them, and re-layouts: 1.81 us -> none  [the longest x1 1.35 us: pair_tile(): jnp.einsum('sic,sje->ijce', left_rows, right_cols, preferred_element_type...]
    convert_element_type x5 -> x0, other arithmetic: 1.66 us -> none  [the longest x1 1.58 us: heed_across_lanes(): return (vertical_pieces.astype(jnp.float32) + update.reshape(seq_count, r...]
  transfers between devices with their start and end apart: 1 -> 0, of which waited for: 1 -> 0; matrix products, arithmetic and copies ran while one was open for 3% -> 0% of each run, Pallas kernels for 0% -> 0%
where the time goes in v1:
time: 22.8 us; the launch traced here: 22.5 us
  Pallas kernels  18.2 us (80%)
  local copies, waits for them, and re-layouts  3.65 us (16%)
  between operations  0.65 us (3%)
    pallas_call x1, Pallas kernels, shards(): pl.pallas_call(functools.partial(kernel, n), out_shape=(jax.ShapeDtypeStr...  18.2 us
    unnamed x5, local copies, waits for them, and re-layouts  3.65 us

profile of v1, /device:TPU:0, one launch (start us, length us, event | category | flops | bytes accessed | tf_op | source)
XLA Modules:
  0.0 22.5 jit_solution(4619057187547445541)
XLA Ops:
  0.6 1.5 %copy.18.wt_ref = bf16[256,64]{1,0:T(8,128)(2,1)} copy(bf16[256,64]{0,1:T(8,128)(2,1)} %param.28) | data formatting | bytes 65536 | tf_op args[12]
  2.1 18.2 %evoformer.1 = (bf16[32,4,256]{2,1,0:T(4,128)(2,1)}, bf16[4,64,128]{2,1,0:T(8,128)(2,1)}) custom-call(bf16[2,64,256]{2,1,0:T(8,128)(2,1)} %x_ref.1, s32[32,64]{1,0:T(8,128)} %occ_ref.1, s32[1,32]{1,0:T(1,128)} %bitcast.15, f32[1,256]{1,0:T(1,128)} %bitcast.9, f32[1,256]{1,0:T(1,128)} %bitcast.10, bf16[256,512]{1,0:T(8,128)(2,1)} %wqk_hbm.1, ...), custom_call_target="tpu_custom_call" | custom-call | tf_op jit(solution)/shard_map/evoformer/pallas_call | solution.py:275
  20.3 0.0 copy-start
  20.3 1.5 %copy.21 = bf16[32,4,256]{2,1,0:T(4,128)(2,1)} copy(bf16[32,4,256]{2,1,0:T(4,128)(2,1)} %get-tuple-element.4) | data formatting | bytes 131072
  21.8 0.0 copy-done
  21.9 0.6 %copy.22 = bf16[4,64,128]{2,1,0:T(8,128)(2,1)} copy(bf16[4,64,128]{2,1,0:T(8,128)(2,1)S(1)} %copy-done) | data formatting | bytes 131072
Async XLA Ops:
  20.3 1.5 %copy-start = (bf16[4,64,128]{2,1,0:T(8,128)(2,1)S(1)}, bf16[4,64,128]{2,1,0:T(8,128)(2,1)}, u32[]{:S(2)}) copy-start(bf16[4,64,128]{2,1,0:T(8,128)(2,1)} %get-tuple-element.5) | copy-start | bytes 196612

commit v2 on v1

--- a/solution.py
+++ b/solution.py
@@ -207,7 +207,7 @@
         revised = after.astype(BF16)
         out_ref[pl.ds(ch * per, per)] = after.reshape(per, local, width).astype(BF16)
         normed = layer_norm(revised.astype(F32), pg_ref[...], pa_ref[...])
-        projected = (dot(normed, wt_ref[...]) + bt_ref[...]) * live_s[at, :]
+        projected = (dot_t(normed, wt_ref[...]) + bt_ref[...]) * live_s[at, :]
         projected = projected.astype(BF16)
         wide = jnp.where(own_seq, dot(projected, spread_e), 0.0).astype(BF16)
         mine = dot(sel, wide)[:local].astype(BF16)
@@ -309,7 +309,7 @@
         ),
         name="evoformer",
     )(x, occ, row(flag), row(ng), row(na), wqk, wvg, row(gb), wo, row(ob),
-      row(pg), row(pa), wt, row(bt), cm, row(cb))
+      row(pg), row(pa), wt.T, row(bt), cm, row(cb))
 
 
 def solution(mesh):

time: 22.8 us -> 21.2 us (0.930)
  local copies, waits for them, and re-layouts: 3.65 us -> 2.16 us
    unnamed x5 -> x4, local copies, waits for them, and re-layouts: 3.65 us -> 2.16 us
where the time goes in v2:
time: 21.2 us; the launch traced here: 21 us
  Pallas kernels  18.2 us (86%)
  local copies, waits for them, and re-layouts  2.16 us (10%)
  between operations  0.65 us (3%)
    pallas_call x1, Pallas kernels, shards(): pl.pallas_call(functools.partial(kernel, n), out_shape=(jax.ShapeDtypeStr...  18.2 us
    unnamed x4, local copies, waits for them, and re-layouts  2.16 us

profile of v2, /device:TPU:0, one launch (start us, length us, event | category | flops | bytes accessed | tf_op | source)
XLA Modules:
  0.0 21.0 jit_solution(7101958221712857846)
XLA Ops:
  0.6 18.2 %evoformer.1 = (bf16[32,4,256]{2,1,0:T(4,128)(2,1)}, bf16[4,64,128]{2,1,0:T(8,128)(2,1)}) custom-call(bf16[2,64,256]{2,1,0:T(8,128)(2,1)} %x_ref.1, s32[32,64]{1,0:T(8,128)} %occ_ref.1, s32[1,32]{1,0:T(1,128)} %bitcast.17, f32[1,256]{1,0:T(1,128)} %bitcast.11, f32[1,256]{1,0:T(1,128)} %bitcast.12, bf16[256,512]{1,0:T(8,128)(2,1)} %wqk_hbm.1, ...), custom_call_target="tpu_custom_call" | custom-call | tf_op jit(solution)/shard_map/evoformer/pallas_call | solution.py:275
  18.8 0.0 copy-start
  18.8 1.5 %copy.20 = bf16[32,4,256]{2,1,0:T(4,128)(2,1)} copy(bf16[32,4,256]{2,1,0:T(4,128)(2,1)} %get-tuple-element.4) | data formatting | bytes 131072
  20.4 0.0 copy-done
  20.4 0.6 %copy.21 = bf16[4,64,128]{2,1,0:T(8,128)(2,1)} copy(bf16[4,64,128]{2,1,0:T(8,128)(2,1)S(1)} %copy-done) | data formatting | bytes 131072
Async XLA Ops:
  18.8 1.5 %copy-start = (bf16[4,64,128]{2,1,0:T(8,128)(2,1)S(1)}, bf16[4,64,128]{2,1,0:T(8,128)(2,1)}, u32[]{:S(2)}) copy-start(bf16[4,64,128]{2,1,0:T(8,128)(2,1)} %get-tuple-element.5) | copy-start | bytes 196612

commit v3 on v2

--- a/solution.py
+++ b/solution.py
@@ -56,31 +56,38 @@
 
 def kernel(
     n,
-    x_ref, occ_ref, flag_ref, ng_ref, na_ref, wqk_hbm, wvg_hbm, gb_ref, wo_hbm, ob_ref,
-    pg_ref, pa_ref, wt_ref, bt_ref, cm_hbm, cb_ref,
+    x_hbm, occ_hbm, flag_hbm, ng_hbm, na_hbm, wqk_hbm, wvg_hbm, gb_hbm, wo_hbm, ob_hbm,
+    pg_hbm, pa_hbm, wt_hbm, bt_hbm, cm_hbm, cb_hbm,
+    out_hbm, pair_hbm,
+    send, recv, rsend, rbuf, cmf, w2,
+    q_s, kb_s, vb_s, g_s, t_s, inv_s, live_s,
+    x_ref, occ_ref, flag_ref, ng_ref, na_ref, wqk, wvg, gb_ref, wo, ob_ref,
+    pg_ref, pa_ref, wt_ref, bt_ref, cm, cb_ref,
     out_ref, pair_ref,
-    send, recv, rsend, rbuf, wqk, wvg, wo, cm, cmf, w2,
-    q_s, kb_s, vb_s, g_s, t_s, inv_s, live_s,
-    wsem, ssem, rsem, ssem2, rsem2,
+    wsem, osem, ssem, rsem, ssem2, rsem2,
 ):
     me = lax.axis_index("dap")
-    own, res, width = x_ref.shape
+    own, res, width = x_hbm.shape
     local = res // n
-    seqs = occ_ref.shape[0]
+    seqs = occ_hbm.shape[0]
     tokens = seqs * local
     chunks = tokens // CHUNK
     per = CHUNK // local
     ke = OUTER_CHANNELS * per
 
+    sources = (
+        x_hbm, occ_hbm, flag_hbm, cm_hbm, ng_hbm, na_hbm, wqk_hbm, wvg_hbm, gb_hbm, wo_hbm,
+        ob_hbm, pg_hbm, pa_hbm, wt_hbm, bt_hbm, cb_hbm,
+    )
+    targets = (
+        x_ref, occ_ref, flag_ref, cm, ng_ref, na_ref, wqk, wvg, gb_ref, wo,
+        ob_ref, pg_ref, pa_ref, wt_ref, bt_ref, cb_ref,
+    )
     loads = [
         pltpu.make_async_copy(src, dst, wsem.at[i])
-        for i, (src, dst) in enumerate(
-            ((cm_hbm, cm), (wqk_hbm, wqk), (wvg_hbm, wvg), (wo_hbm, wo))
-        )
+        for i, (src, dst) in enumerate(zip(sources, targets))
     ]
-    for load in loads:
-        load.start()
-
+    loads[0].start()
     barrier = pltpu.get_barrier_semaphore()
 
     def greet(k):
@@ -89,6 +96,9 @@
         )
 
     each_peer(n, greet)
+    for load in loads[1:]:
+        load.start()
+    loads[0].wait()
 
     x32 = x_ref[...].astype(F32)
     for p in range(n):
@@ -111,6 +121,8 @@
 
     each_peer(n, post)
 
+    loads[1].wait()
+    loads[2].wait()
     occ = occ_ref[...].astype(F32)
     flag = flag_ref[...].astype(F32)
     pick = (iota((8, res), 1) == me * local + iota((8, res), 0)).astype(F32)
@@ -139,7 +151,7 @@
 
     repeat(chunks, live_column)
 
-    loads[0].wait()
+    loads[3].wait()
     cmf[...] = cm[...].astype(F32)
     for e in range(OUTER_CHANNELS):
         w2[0:OUTER_CHANNELS, e * PAIR_DIM : (e + 1) * PAIR_DIM] = cmf[
@@ -158,7 +170,7 @@
     ).astype(BF16)
     lane_head = iota((CHUNK, width), 1) // HEAD_CHANNELS
 
-    for load in loads[1:]:
+    for load in loads[4:]:
         load.wait()
     pltpu.make_async_copy(recv.at[pl.ds(0, n - 1)], recv.at[pl.ds(0, n - 1)], rsem).wait()
 
@@ -241,6 +253,8 @@
         each_peer(n, post)
 
     repeat(chunks, attend)
+    out_copy = pltpu.make_async_copy(out_ref, out_hbm, osem.at[0])
+    out_copy.start()
     if chunks > 1:
         post_right()
 
@@ -256,9 +270,12 @@
         pair_ref[i] = (
             total[:, i * PAIR_DIM : (i + 1) * PAIR_DIM] * inv[:, i : i + 1] + cb_ref[...]
         ).astype(BF16)
-
+    pair_copy = pltpu.make_async_copy(pair_ref, pair_hbm, osem.at[1])
+    pair_copy.start()
     pltpu.make_async_copy(send.at[pl.ds(0, n - 1)], send.at[pl.ds(0, n - 1)], ssem).wait()
     pltpu.make_async_copy(rbuf.at[pl.ds(0, n - 1)], rbuf.at[pl.ds(0, n - 1)], ssem2).wait()
+    out_copy.wait()
+    pair_copy.wait()
 
 
 def shards(n, *args):
@@ -270,25 +287,25 @@
     chunks = tokens // CHUNK
     ke = OUTER_CHANNELS * (CHUNK // local)
     row = lambda v: v.reshape(1, -1)
-    vm = pl.BlockSpec(memory_space=pltpu.VMEM)
+    operands = (
+        x, occ, row(flag), row(ng), row(na), wqk, wvg, row(gb), wo, row(ob),
+        row(pg), row(pa), wt.T, row(bt), cm, row(cb),
+    )
+    outs = (
+        jax.ShapeDtypeStruct((seqs, local, width), BF16),
+        jax.ShapeDtypeStruct((local, res, PAIR_DIM), BF16),
+    )
     hbm = pl.BlockSpec(memory_space=pl.ANY)
     return pl.pallas_call(
         functools.partial(kernel, n),
-        out_shape=(
-            jax.ShapeDtypeStruct((seqs, local, width), BF16),
-            jax.ShapeDtypeStruct((local, res, PAIR_DIM), BF16),
-        ),
-        in_specs=[vm, vm, vm, vm, vm, hbm, hbm, vm, hbm, vm, vm, vm, vm, vm, hbm, vm],
-        out_specs=(vm, vm),
+        out_shape=outs,
+        in_specs=[hbm] * len(operands),
+        out_specs=(hbm, hbm),
         scratch_shapes=[
             pltpu.VMEM((n, own * local, width), BF16),
             pltpu.VMEM((n, own * local, width), BF16),
             pltpu.VMEM((local, chunks * ke), BF16),
             pltpu.VMEM((n, local, chunks * ke), BF16),
-            pltpu.VMEM(wqk.shape, BF16),
-            pltpu.VMEM(wvg.shape, BF16),
-            pltpu.VMEM(wo.shape, BF16),
-            pltpu.VMEM(cm.shape, BF16),
             pltpu.VMEM(cm.shape, F32),
             pltpu.VMEM((2 * OUTER_CHANNELS, OUTER_CHANNELS * PAIR_DIM), BF16),
             pltpu.VMEM((tokens, width), BF16),
@@ -298,7 +315,9 @@
             pltpu.VMEM((chunks, ke, local * PAIR_DIM), BF16),
             pltpu.VMEM((res, 8), F32),
             pltpu.VMEM((tokens, 1), F32),
-            pltpu.SemaphoreType.DMA((4,)),
+            *[pltpu.VMEM(v.shape, v.dtype) for v in operands + outs],
+            pltpu.SemaphoreType.DMA((len(operands),)),
+            pltpu.SemaphoreType.DMA((2,)),
             pltpu.SemaphoreType.DMA,
             pltpu.SemaphoreType.DMA,
             pltpu.SemaphoreType.DMA,
@@ -308,8 +327,7 @@
             collective_id=0, has_side_effects=True, vmem_limit_bytes=60 * 1024 * 1024
         ),
         name="evoformer",
-    )(x, occ, row(flag), row(ng), row(na), wqk, wvg, row(gb), wo, row(ob),
-      row(pg), row(pa), wt.T, row(bt), cm, row(cb))
+    )(*operands)
 
 
 def solution(mesh):

time: 21.2 us -> 20.3 us (0.958)
  Pallas kernels: 18.2 us -> 17.3 us
    pallas_call x1, Pallas kernels: 18.2 us -> 17.3 us  [shards(): pl.pallas_call(functools.partial(kernel, n), out_shape=outs, in_specs=[hb...]
where the time goes in v3:
time: 20.3 us; the launch traced here: 20.1 us
  Pallas kernels  17.3 us (85%)
  local copies, waits for them, and re-layouts  2.16 us (11%)
  between operations  0.65 us (3%)
    pallas_call x1, Pallas kernels, shards(): pl.pallas_call(functools.partial(kernel, n), out_shape=outs, in_specs=[hb...  17.3 us
    unnamed x4, local copies, waits for them, and re-layouts  2.16 us

profile of v3, /device:TPU:0, one launch (start us, length us, event | category | flops | bytes accessed | tf_op | source)
XLA Modules:
  0.0 20.1 jit_solution(12121196082323869942)
XLA Ops:
  0.6 17.3 %evoformer.1 = (bf16[32,4,256]{2,1,0:T(4,128)(2,1)}, bf16[4,64,128]{2,1,0:T(8,128)(2,1)}) custom-call(bf16[2,64,256]{2,1,0:T(8,128)(2,1)} %x_hbm.1, s32[32,64]{1,0:T(8,128)} %occ_hbm.1, s32[1,32]{1,0:T(1,128)} %bitcast.17, f32[1,256]{1,0:T(1,128)} %bitcast.11, f32[1,256]{1,0:T(1,128)} %bitcast.12, bf16[256,512]{1,0:T(8,128)(2,1)} %wqk_hbm.1, ...), custom_call_target="tpu_custom_call" | custom-call | tf_op jit(solution)/shard_map/evoformer/pallas_call | solution.py:299
  18.0 0.0 copy-start
  18.0 1.5 %copy.20 = bf16[32,4,256]{2,1,0:T(4,128)(2,1)} copy(bf16[32,4,256]{2,1,0:T(4,128)(2,1)} %get-tuple-element.4) | data formatting | bytes 131072
  19.5 0.0 copy-done
  19.5 0.6 %copy.21 = bf16[4,64,128]{2,1,0:T(8,128)(2,1)} copy(bf16[4,64,128]{2,1,0:T(8,128)(2,1)S(1)} %copy-done) | data formatting | bytes 131072
Async XLA Ops:
  18.0 1.5 %copy-start = (bf16[4,64,128]{2,1,0:T(8,128)(2,1)S(1)}, bf16[4,64,128]{2,1,0:T(8,128)(2,1)}, u32[]{:S(2)}) copy-start(bf16[4,64,128]{2,1,0:T(8,128)(2,1)} %get-tuple-element.5) | copy-start | bytes 196612

commit v4 on v3

--- a/solution.py
+++ b/solution.py
@@ -48,10 +48,18 @@
 
 def each_peer(n, body):
     if n <= 16:
-        for k in range(1, n):
+        for k in range(n - 1):
             body(k)
     else:
-        lax.fori_loop(1, n, lambda k, c: (body(k), c)[1], 0)
+        lax.fori_loop(0, n - 1, lambda k, c: (body(k), c)[1], 0)
+
+
+def far_first(me, n, k):
+    upper = lax.div(me, n // 2)
+    high = n - 1 - k
+    high = high - lax.div(me - high + n, n)
+    low = k + lax.div(k - me + n, n)
+    return upper * low + (1 - upper) * high
 
 
 def kernel(
@@ -92,7 +100,7 @@
 
     def greet(k):
         pl.semaphore_signal(
-            barrier, inc=1, device_id={"dap": lax.rem(me + k, n)}, device_id_type=MESH
+            barrier, inc=1, device_id={"dap": far_first(me, n, k)}, device_id_type=MESH
         )
 
     each_peer(n, greet)
@@ -109,7 +117,7 @@
     pl.semaphore_wait(barrier, n - 1)
 
     def post(k):
-        peer = lax.rem(me + k, n)
+        peer = far_first(me, n, k)
         pltpu.make_async_remote_copy(
             src_ref=send.at[peer],
             dst_ref=recv.at[me],
@@ -246,7 +254,7 @@
                 dst_ref=rbuf.at[me],
                 send_sem=ssem2,
                 recv_sem=rsem2,
-                device_id={"dap": lax.rem(me + k, n)},
+                device_id={"dap": far_first(me, n, k)},
                 device_id_type=MESH,
             ).start()
 
@@ -278,6 +286,11 @@
     pair_copy.wait()
 
 
+def hand_over(a_ref, b_ref, c_ref, d_ref):
+    c_ref[...] = a_ref[...]
+    d_ref[...] = b_ref[...]
+
+
 def shards(n, *args):
     x, occ, flag, ng, na, wqk, wvg, gb, wo, ob, pg, pa, wt, bt, cm, cb = args
     own, res, width = x.shape
@@ -296,7 +309,7 @@
         jax.ShapeDtypeStruct((local, res, PAIR_DIM), BF16),
     )
     hbm = pl.BlockSpec(memory_space=pl.ANY)
-    return pl.pallas_call(
+    results = pl.pallas_call(
         functools.partial(kernel, n),
         out_shape=outs,
         in_specs=[hbm] * len(operands),
@@ -328,6 +341,10 @@
         ),
         name="evoformer",
     )(*operands)
+    vm = pl.BlockSpec(memory_space=pltpu.VMEM)
+    return pl.pallas_call(
+        hand_over, out_shape=outs, in_specs=[vm, vm], out_specs=(vm, vm), name="hand_over"
+    )(*results)
 
 
 def solution(mesh):

time: 20.3 us -> 19.2 us (0.946)
  local copies, waits for them, and re-layouts: 2.16 us -> 0 us
  Pallas kernels: 17.3 us -> 18.4 us
    unnamed x4 -> x0, local copies, waits for them, and re-layouts: 2.16 us -> none
    pallas_call x0 -> x1, Pallas kernels: none -> 1.53 us  [shards(): pl.pallas_call(hand_over, out_shape=outs, in_specs=[vm, vm], out_specs=(v...]
    pallas_call x1, Pallas kernels: 17.3 us -> 16.8 us  [shards(): pl.pallas_call(functools.partial(kernel, n), out_shape=outs, in_specs=[hb...]
where the time goes in v4:
time: 19.2 us; the launch traced here: 19 us
  Pallas kernels  18.4 us (96%)
  between operations  0.64 us (3%)
    pallas_call x1, Pallas kernels, shards(): pl.pallas_call(functools.partial(kernel, n), out_shape=outs, in_specs=[hb...  16.8 us
    pallas_call x1, Pallas kernels, shards(): pl.pallas_call(hand_over, out_shape=outs, in_specs=[vm, vm], out_specs=(v...  1.53 us

profile of v4, /device:TPU:0, one launch (start us, length us, event | category | flops | bytes accessed | tf_op | source)
XLA Modules:
  0.0 19.0 jit_solution(6403023369006354242)
XLA Ops:
  0.6 16.8 %evoformer.1 = (bf16[32,4,256]{2,1,0:T(4,128)(2,1)}, bf16[4,64,128]{2,1,0:T(8,128)(2,1)}) custom-call(bf16[2,64,256]{2,1,0:T(8,128)(2,1)} %x_hbm.1, s32[32,64]{1,0:T(8,128)} %occ_hbm.1, s32[1,32]{1,0:T(1,128)} %bitcast.17, f32[1,256]{1,0:T(1,128)} %bitcast.11, f32[1,256]{1,0:T(1,128)} %bitcast.12, bf16[256,512]{1,0:T(8,128)(2,1)} %wqk_hbm.1, ...), custom_call_target="tpu_custom_call" | custom-call | tf_op jit(solution)/shard_map/evoformer/pallas_call | solution.py:312
  17.5 1.5 %hand_over.1 = (bf16[32,4,256]{2,1,0:T(4,128)(2,1)}, bf16[4,64,128]{2,1,0:T(8,128)(2,1)}) custom-call(bf16[32,4,256]{2,1,0:T(4,128)(2,1)} %get-tuple-element.4.a_ref, bf16[4,64,128]{2,1,0:T(8,128)(2,1)} %get-tuple-element.5.b_ref), custom_call_target="tpu_custom_call" | custom-call | tf_op jit(solution)/shard_map/hand_over/pallas_call | solution.py:345
